TPU v7x, 32 devices: a whole 2x2x4 slice. The times are simulated.
32 devices in a mesh: cp: 16 (over z, y, core), vocab: 2 (over x).
Axes of the slice: x: 2, y: 2, z: 4, core: 2. Of those that a mesh axis runs over, the one named last changes fastest.
Arguments:
- queries: bfloat16 [2048, 4096], P('cp', 'vocab'), may hold values from -160 to 160
- key_states: bfloat16 [2048, 1024], P('cp', 'vocab'), may hold values from -6 to 6
- value_states: bfloat16 [2048, 1024], P('cp', 'vocab'), may hold values from -6 to 6
- out_grad: bfloat16 [2048, 4096], P('cp', 'vocab'), may hold values from -6 to 6
- o_weight: bfloat16 [4096, 4096], P('vocab'), may hold values from -0.09375 to 0.09375
- span_order: int32 [32], replicated, may hold values from 0 to 31, each once
Outputs:
- query_grad: float32 [2048, 4096], P('cp', 'vocab')
- key_grad: float32 [2048, 1024], P('cp', 'vocab')
- value_grad: float32 [2048, 1024], P('cp', 'vocab')
Inputs may be any that keep to these rules, and one draw needn't show every extreme that they name: `span_order`: each of the 32 span indices once.
All inputs are finite; a program needn't handle non-finite values.
Results may differ from a plain program's by a relative error of at most 0.014.
Values may be sent and summed in bfloat16 or wider, within the bound.
A program may use at most 64 MiB of HBM per device.

v0:
```python
import jax
import jax.numpy as jnp
from jax import lax
from jax.sharding import PartitionSpec as P

HEADS = 32
KV_HEADS = 8
HEAD_DIM = 128


def positions(span_order, span_rows):
    offsets = jnp.arange(span_rows, dtype=jnp.int32)
    return (span_order[:, None] * span_rows + offsets[None, :]).reshape(-1)


def block_scores(query_block, key_block, query_places, key_places, factor):
    scores = (
        jnp.einsum("qkgd,skd->kgqs", query_block, key_block, preferred_element_type=jnp.float32)
        * factor
    )
    visible = key_places[None, :] <= query_places[:, None]
    return jnp.where(visible, scores, -jnp.inf)


def local(queries, key_states, value_states, out_grad, o_weight, span_order):
    own_rows = queries.shape[0]
    kv_width = key_states.shape[1]
    kv_heads = kv_width // HEAD_DIM
    groups = HEADS // KV_HEADS
    factor = HEAD_DIM ** (-0.5)
    upstream = lax.dot_general(
        lax.all_gather(out_grad, "vocab", axis=1, tiled=True),
        o_weight,
        (((1,), (1,)), ((), ())),
        preferred_element_type=jnp.float32,
    ).astype(jnp.bfloat16)
    places = positions(span_order, own_rows // 2)
    seq_len = places.shape[0]
    own_places = lax.dynamic_slice_in_dim(places, lax.axis_index("cp") * own_rows, own_rows, 0)
    query_heads = queries.reshape(own_rows, kv_heads, groups, HEAD_DIM)
    upstream_heads = upstream.reshape(own_rows, kv_heads, groups, HEAD_DIM)
    key_all, value_all = (
        lax.all_gather(key_states, "cp", axis=0, tiled=True),
        lax.all_gather(value_states, "cp", axis=0, tiled=True),
    )
    key_all = key_all.reshape(seq_len, kv_heads, HEAD_DIM)
    value_all = value_all.reshape(seq_len, kv_heads, HEAD_DIM)
    block_rows = own_rows * 8
    block_count = seq_len // block_rows
    block_ids = jnp.arange(block_count, dtype=jnp.int32)
    stat_shape = (kv_heads, groups, own_rows)

    def key_block(block_index):
        offset = block_index * block_rows
        return (
            lax.dynamic_slice_in_dim(key_all, offset, block_rows, 0),
            lax.dynamic_slice_in_dim(value_all, offset, block_rows, 0),
            lax.dynamic_slice_in_dim(places, offset, block_rows, 0),
        )

    def stats_step(carried, block_index):
        running, totals, delta_acc = carried
        keys_now, values_now, places_now = key_block(block_index)
        scores = block_scores(query_heads, keys_now, own_places, places_now, factor)
        newest = jnp.maximum(running, jnp.max(scores, axis=3))
        rescale = jnp.exp(running - newest)
        raised = jnp.exp(scores - newest[..., None])
        grad_probs = jnp.einsum(
            "qkgd,skd->kgqs", upstream_heads, values_now, preferred_element_type=jnp.float32
        )
        totals = totals * rescale + jnp.sum(raised, axis=3)
        delta_acc = delta_acc * rescale + jnp.sum(raised * grad_probs, axis=3)
        return ((newest, totals, delta_acc), None)

    start_stats = (
        jnp.full(stat_shape, -1e30, jnp.float32),
        jnp.zeros(stat_shape, jnp.float32),
        jnp.zeros(stat_shape, jnp.float32),
    )
    (running, totals, delta_acc), unused = lax.scan(stats_step, start_stats, block_ids)
    logsum = running + jnp.log(totals)
    deltas = delta_acc / totals

    def grad_pieces(block_index):
        keys_now, values_now, places_now = key_block(block_index)
        scores = block_scores(query_heads, keys_now, own_places, places_now, factor)
        weights = jnp.exp(scores - logsum[..., None])
        grad_probs = jnp.einsum(
            "qkgd,skd->kgqs", upstream_heads, values_now, preferred_element_type=jnp.float32
        )
        grad_scores = (weights * (grad_probs - deltas[..., None])).astype(jnp.bfloat16)
        return (keys_now, weights, grad_scores)

    query_zeros = jnp.zeros((own_rows, kv_heads, groups, HEAD_DIM), jnp.float32)

    def grad_step(carried, block_index):
        keys_now, weights, grad_scores = grad_pieces(block_index)
        carried = (
            carried
            + jnp.einsum(
                "kgqs,skd->qkgd", grad_scores, keys_now, preferred_element_type=jnp.float32
            )
            * factor
        )
        key_term = (
            jnp.einsum(
                "kgqs,qkgd->skd", grad_scores, query_heads, preferred_element_type=jnp.float32
            )
            * factor
        )
        value_term = jnp.einsum(
            "kgqs,qkgd->skd",
            weights.astype(jnp.bfloat16),
            upstream_heads,
            preferred_element_type=jnp.float32,
        )
        joined = jnp.concatenate(
            (key_term.reshape(block_rows, kv_width), value_term.reshape(block_rows, kv_width)),
            axis=1,
        )
        return (carried, joined)

    query_total, stacked = lax.scan(grad_step, query_zeros, block_ids)
    terms = stacked.reshape(seq_len, 2 * kv_width)
    mine = lax.psum_scatter(
        terms.astype(jnp.bfloat16), "cp", scatter_dimension=0, tiled=True
    ).astype(jnp.float32)
    key_grad = mine[:, :kv_width]
    value_grad = mine[:, kv_width:]
    query_grad = query_total.reshape(own_rows, kv_heads * groups * HEAD_DIM)
    return (query_grad, key_grad, value_grad)


def solution(mesh):
    return jax.shard_map(
        local,
        mesh=mesh,
        in_specs=(
            P("cp", "vocab"),
            P("cp", "vocab"),
            P("cp", "vocab"),
            P("cp", "vocab"),
            P("vocab", None),
            P(),
        ),
        out_specs=(P("cp", "vocab"), P("cp", "vocab"), P("cp", "vocab")),
        check_vma=False,
    )
```

profile of v0, /device:TPU:15, one launch (start us, length us, event | category | flops | bytes accessed | tf_op | source)
XLA Modules:
  0.0 250.3 jit_solution(16052969904517764224)
XLA Ops:
  14.7 16.1 %all-gather.8.cloned.1.call-done = bf16[128,4096]{1,0:T(8,128)(2,1)} async-done(((bf16[128,2048]{1,0:T(8,128)(2,1)}), bf16[128,4096]{1,0:T(8,128)(2,1)}) %all-gather.8.cloned.1.call-update) | async-done | bytes 1048592 | tf_op jit(solution)/shard_map/all_gather | solution.py:32
  30.8 11.7 %convolution_convert_fusion = bf16[128,2048]{1,0:T(8,128)(2,1)S(1)} fusion(bf16[128,4096]{1,0:T(8,128)(2,1)} %all-gather.8.cloned.1.call-done, bf16[2048,4096]{1,0:T(8,128)(2,1)} %param.14), kind=kOutput, calls=%fused_computation.51 | convolution fusion | flops 2147745792 | bytes 18350080 | tf_op jit(solution)/shard_map/dot_general | solution.py:31
  45.2 30.7 %all-gather.4.cloned.1.call-done = bf16[2048,512]{0,1:T(8,128)(2,1)} async-done(((bf16[128,512]{0,1:T(8,128)(2,1)}), bf16[2048,512]{0,1:T(8,128)(2,1)}) %all-gather.4.cloned.1.call-update) | async-done | bytes 2097168 | tf_op jit(solution)/shard_map/all_gather | solution.py:43
  75.9 3.0 %copy.34 = bf16[2048,4,128]{2,0,1:T(8,128)(2,1)S(1)} copy(bf16[2048,4,128]{0,2,1:T(8,128)(2,1)} %bitcast.158) | data formatting | bytes 4194304
  78.9 39.9 %all-gather.6.cloned.1.call-done = bf16[2048,512]{0,1:T(8,128)(2,1)} async-done(((bf16[128,512]{0,1:T(8,128)(2,1)}), bf16[2048,512]{0,1:T(8,128)(2,1)}) %all-gather.6.cloned.1.call-update) | async-done | bytes 2097168 | tf_op jit(solution)/shard_map/all_gather | solution.py:44
  118.8 4.0 %copy.32 = bf16[2048,4,128]{2,0,1:T(8,128)(2,1)} copy(bf16[2048,4,128]{0,2,1:T(8,128)(2,1)} %bitcast.159) | data formatting | bytes 4194304
  122.7 16.3 %while.28 = (s32[]{:T(128)}, f32[4,4,128]{2,1,0:T(4,128)S(1)}, f32[4,4,128]{2,1,0:T(4,128)S(1)}, f32[4,4,128]{2,1,0:T(4,128)S(1)}, s32[2]{0:T(128)S(1)}, /*index...) while((s32[]{:T(128)}, f32[4,4,128]{2,1,0:T(4,128)S(1)}, ...), condition=%wide.region_4.5_spmd.clone, body=%wide.region_0.4_spmd.clone.sunk | while | flops 1099053056 | bytes 39482140 | solution.py:80
  124.2 2.4 fusion.75
  126.7 2.4 fusion.76
  129.1 1.7 fusion.77
  132.4 2.4 fusion.75
  134.9 2.4 fusion.76
  139.1 26.7 %while.29 = (s32[]{:T(128)}, f32[128,4,4,128]{0,3,2,1:T(8,128)S(1)}, bf16[2,1024,1024]{1,2,0:T(8,128)(2,1)}, s32[2]{0:T(128)S(1)}, bf16[2048,4,128]{2,0,1:T(8,12...) while((s32[]{:T(128)}, ...), condition=%wide.region_6.7_spmd.clone, body=%wide.region_5.6_spmd.clone.sunk | while | flops 2711486464 | bytes 97948544 | solution.py:123
  140.6 2.3 fusion.89
  142.9 2.1 fusion.92
  145.0 2.5 %fusion.90 = bf16[4,4,128,1024]{2,3,1,0:T(8,128)(2,1)S(1)} fusion(f32[4,1024,128,4]{2,1,3,0:T(8,128)S(1)} %fusion.89, f32[4,4,128]{2,1,0:T(4,128)S(1)} %get-tuple-element.543, f32[4,4,128]{2,1,0:T(4,128)S(1)} %get-tuple-element.540, pred[128,1024]{0,1:T(8,128)(4,1)S(1)} %broadcast_compare_fusion.5, bf16[128,4,4,128]{0,3,2,1:T(8,128)(2,1)S(1)} %copy-done.6, ...), kind=kOutput, calls=%fused_computation.22.clone.1 | convolution fusion | flops 549453824 | bytes 14303236 | tf_op jit(solution)/shard_map/while/body/eval_jaxpr/qkgd,skd->kgqs/dot_general | solution.py:88
  150.5 1.9 copy-done.3
  153.9 2.3 fusion.89
  156.2 2.1 fusion.92
  158.4 2.5 %fusion.90 = bf16[4,4,128,1024]{2,3,1,0:T(8,128)(2,1)S(1)} fusion(f32[4,1024,128,4]{2,1,3,0:T(8,128)S(1)} %fusion.89, f32[4,4,128]{2,1,0:T(4,128)S(1)} %get-tuple-element.543, f32[4,4,128]{2,1,0:T(4,128)S(1)} %get-tuple-element.540, pred[128,1024]{0,1:T(8,128)(4,1)S(1)} %broadcast_compare_fusion.5, bf16[128,4,4,128]{0,3,2,1:T(8,128)(2,1)S(1)} %copy-done.6, ...), kind=kOutput, calls=%fused_computation.22.clone.1 | convolution fusion | flops 549453824 | bytes 14303236 | tf_op jit(solution)/shard_map/while/body/eval_jaxpr/qkgd,skd->kgqs/dot_general | solution.py:88
  163.8 1.9 copy-done.3
  165.7 6.2 %copy.38 = bf16[2,1024,1024]{2,1,0:T(8,128)(2,1)} copy(bf16[2,1024,1024]{1,2,0:T(8,128)(2,1)} %get-tuple-element.129) | data formatting | bytes 8388608 | tf_op jit(solution)/shard_map/convert_element_type | solution.py:126
  173.3 68.6 %reduce-scatter.2.cloned.1.call-done = bf16[128,1024]{1,0:T(8,128)(2,1)} async-done(((bf16[2048,1024]{1,0:T(8,128)(2,1)}), bf16[128,1024]{1,0:T(8,128)(2,1)}) %reduce-scatter.2.cloned.1.call-update) | async-done | bytes 262160 | tf_op jit(solution)/shard_map/reduce_scatter | solution.py:125
  241.9 1.8 fusion.38
  (81 shorter events, 22.0 us)
Async XLA Ops:
  7.2 23.7 %all-gather.8.cloned.1.call-start = ((), (), s32[]{:S(2)}) async-start(), calls=%async_computation.3 | async-start | bytes 1572864 | tf_op jit(solution)/shard_map/all_gather | solution.py:32
  7.9 68.0 %all-gather.4.cloned.1.call-start = ((), (), s32[]{:S(2)}) async-start(), calls=%async_computation.1 | async-start | bytes 2228224 | tf_op jit(solution)/shard_map/all_gather | solution.py:43
  9.6 109.1 %all-gather.6.cloned.1.call-start = ((), (), s32[]{:S(2)}) async-start(), calls=%async_computation.2 | async-start | bytes 2228224 | tf_op jit(solution)/shard_map/all_gather | solution.py:44
  11.4 230.5 %reduce-scatter.2.cloned.1.call-start = ((), (), s32[]{:S(2)}) async-start(), calls=%async_computation.4 | async-start | bytes 4456448 | tf_op jit(solution)/shard_map/reduce_scatter | solution.py:125
  13.6 29.0 %copy-start = (bf16[128,2048]{0,1:T(8,128)(2,1)}, bf16[128,2048]{0,1:T(8,128)(2,1)S(1)}, u32[]{:S(2)}) copy-start(bf16[128,2048]{0,1:T(8,128)(2,1)S(1)} %copy.28) | copy-start | bytes 1572868
  124.0 2.7 %copy-start.4 = (bf16[2048,4,128]{2,0,1:T(8,128)(2,1)S(1)}, bf16[2048,4,128]{2,0,1:T(8,128)(2,1)}, u32[]{:S(2)}) copy-start(bf16[2048,4,128]{2,0,1:T(8,128)(2,1)} %get-tuple-element.494) | copy-start | bytes 6291460 | tf_op jit(solution)/shard_map/while
  124.0 2.7 %copy-start.7 = (bf16[128,4,4,128]{3,0,2,1:T(8,128)(2,1)S(1)}, bf16[128,4,4,128]{3,0,2,1:T(8,128)(2,1)}, u32[]{:S(2)}) copy-start(bf16[128,4,4,128]{3,0,2,1:T(8,128)(2,1)} %get-tuple-element.495) | copy-start | bytes 1572868 | tf_op jit(solution)/shard_map/while
  132.1 2.7 %copy-start.4 = (bf16[2048,4,128]{2,0,1:T(8,128)(2,1)S(1)}, bf16[2048,4,128]{2,0,1:T(8,128)(2,1)}, u32[]{:S(2)}) copy-start(bf16[2048,4,128]{2,0,1:T(8,128)(2,1)} %get-tuple-element.494) | copy-start | bytes 6291460 | tf_op jit(solution)/shard_map/while
  132.1 2.7 %copy-start.7 = (bf16[128,4,4,128]{3,0,2,1:T(8,128)(2,1)S(1)}, bf16[128,4,4,128]{3,0,2,1:T(8,128)(2,1)}, u32[]{:S(2)}) copy-start(bf16[128,4,4,128]{3,0,2,1:T(8,128)(2,1)} %get-tuple-element.495) | copy-start | bytes 1572868 | tf_op jit(solution)/shard_map/while
  140.3 2.5 %copy-start.6 = (bf16[128,4,4,128]{0,3,2,1:T(8,128)(2,1)S(1)}, bf16[128,4,4,128]{0,3,2,1:T(8,128)(2,1)}, u32[]{:S(2)}) copy-start(bf16[128,4,4,128]{0,3,2,1:T(8,128)(2,1)} %get-tuple-element.542) | copy-start | bytes 1572868 | tf_op jit(solution)/shard_map/while
  142.9 2.2 copy-start.5
  145.0 3.6 %copy-start.1 = (bf16[128,4,4,128]{0,3,2,1:T(8,128)(2,1)S(1)}, bf16[128,4,4,128]{0,3,2,1:T(8,128)(2,1)}, u32[]{:S(2)}) copy-start(bf16[128,4,4,128]{0,3,2,1:T(8,128)(2,1)} %get-tuple-element.539) | copy-start | bytes 1572868 | tf_op jit(solution)/shard_map/while
  147.6 2.6 %copy-start.2 = (bf16[2,1024,1024]{1,2,0:T(8,128)(2,1)S(1)}, bf16[2,1024,1024]{1,2,0:T(8,128)(2,1)}, u32[]{:S(2)}) copy-start(bf16[2,1024,1024]{1,2,0:T(8,128)(2,1)} %get-tuple-element.518) | copy-start | bytes 12582916 | tf_op jit(solution)/shard_map/while
  150.5 1.9 copy-start.3
  153.7 2.5 %copy-start.6 = (bf16[128,4,4,128]{0,3,2,1:T(8,128)(2,1)S(1)}, bf16[128,4,4,128]{0,3,2,1:T(8,128)(2,1)}, u32[]{:S(2)}) copy-start(bf16[128,4,4,128]{0,3,2,1:T(8,128)(2,1)} %get-tuple-element.542) | copy-start | bytes 1572868 | tf_op jit(solution)/shard_map/while
  156.2 2.2 copy-start.5
  158.4 3.6 %copy-start.1 = (bf16[128,4,4,128]{0,3,2,1:T(8,128)(2,1)S(1)}, bf16[128,4,4,128]{0,3,2,1:T(8,128)(2,1)}, u32[]{:S(2)}) copy-start(bf16[128,4,4,128]{0,3,2,1:T(8,128)(2,1)} %get-tuple-element.539) | copy-start | bytes 1572868 | tf_op jit(solution)/shard_map/while
  160.9 2.6 %copy-start.2 = (bf16[2,1024,1024]{1,2,0:T(8,128)(2,1)S(1)}, bf16[2,1024,1024]{1,2,0:T(8,128)(2,1)}, u32[]{:S(2)}) copy-start(bf16[2,1024,1024]{1,2,0:T(8,128)(2,1)} %get-tuple-element.518) | copy-start | bytes 12582916 | tf_op jit(solution)/shard_map/while
  163.8 1.9 copy-start.3
Sparse Core Ops, SparseCore 0:
  9.5 21.2 all-gather.7
  33.6 42.2 all-gather.3
  78.6 40.1 all-gather.5
  172.1 69.7 reduce-scatter.1
where the time goes:
time: 254 us; the launch traced here: 250 us
  waiting for transfers between devices  156 us (61%)
  matrix products  40.6 us (16%)
  local copies, waits for them, and re-layouts  31.1 us (12%)
  between operations  13.9 us (5%)
  other arithmetic  5.53 us (2%)
  loops' own time  3.08 us (1%)
    reduce_scatter x1, waiting for transfers between devices, local(): lax.psum_scatter(terms.astype(jnp.bfloat16), 'cp', scatter_dimension=0, t...  68.6 us
    all_gather x1, waiting for transfers between devices, local(): lax.all_gather(value_states, 'cp', axis=0, tiled=True)  39.9 us
    all_gather x1, waiting for transfers between devices, local(): lax.all_gather(key_states, 'cp', axis=0, tiled=True)  30.7 us
    all_gather x1, waiting for transfers between devices, local(): lax.all_gather(out_grad, 'vocab', axis=1, tiled=True)  16.1 us
    unnamed x10, local copies, waits for them, and re-layouts  14.9 us
    dot_general x1, matrix products, local(): lax.dot_general(lax.all_gather(out_grad, 'vocab', axis=1, tiled=True), o_...  11.7 us
    dot_general x4, matrix products, block_scores(): jnp.einsum('qkgd,skd->kgqs', query_block, key_block, preferred_element_ty...  9.46 us
    convert_element_type x1, local copies, waits for them, and re-layouts, local(): terms.astype(jnp.bfloat16)  6.24 us
  transfers between devices with their start and end apart: 4, of which 4 were waited for; matrix products, arithmetic and copies ran while one was open for 10% of the time, Pallas kernels for 0%

commit v1 on v0

--- a/solution.py
+++ b/solution.py
@@ -1,6 +1,10 @@
+import functools
+
 import jax
 import jax.numpy as jnp
 from jax import lax
+from jax.experimental import pallas as pl
+from jax.experimental.pallas import tpu as pltpu
 from jax.sharding import PartitionSpec as P
 
 HEADS = 32
@@ -131,9 +135,354 @@
     return (query_grad, key_grad, value_grad)
 
 
+MESH = pl.DeviceIdType.MESH
+NT = (((1,), (1,)), ((), ()))
+NN = (((1,), (0,)), ((), ()))
+TILE = 256
+
+
+def dot(a, b, dims):
+    return lax.dot_general(a, b, dims, preferred_element_type=jnp.float32)
+
+
+def greet(peers):
+    barrier = pltpu.get_barrier_semaphore()
+    for peer in peers:
+        pl.semaphore_signal(barrier, inc=1, device_id=peer, device_id_type=MESH)
+    pl.semaphore_wait(barrier, len(peers))
+
+
+def send_kernel(
+    n, groups, q_ref, k_ref, v_ref, g_ref, w_ref, q_all, k_all, v_all, u_all,
+    own_g, other_g, own_w, other_w, partial, u_buf,
+    send_sem, recv_sem, own_sem, w_sem, g_sem, gx_sem,
+):
+    me = lax.axis_index("cp")
+    half = lax.axis_index("vocab")
+    pairs = n // 2
+    width = g_ref.shape[1]
+    two = 2 * HEAD_DIM
+
+    def w_copy(t, own):
+        pair = lax.rem(me // 2 + t, pairs)
+        side = half if own else 1 - half
+        return pltpu.make_async_copy(
+            w_ref.at[
+                pl.ds(pl.multiple_of(pair * two, two), two),
+                pl.ds(pl.multiple_of(side * width, width), width),
+            ],
+            (own_w if own else other_w).at[t],
+            w_sem.at[0 if own else 1, t],
+        )
+
+    own_g_copy = pltpu.make_async_copy(g_ref, own_g, g_sem)
+    own_g_copy.start()
+    order = list(range(1, pairs)) + [0]
+    for t in order:
+        w_copy(t, True).start()
+    for t in order:
+        w_copy(t, False).start()
+
+    greet([{"cp": lax.rem(me + s, n)} for s in range(1, n)] + [{"vocab": 1 - half}])
+
+    g_copy = pltpu.make_async_remote_copy(
+        src_ref=g_ref, dst_ref=other_g, send_sem=gx_sem.at[0], recv_sem=gx_sem.at[1],
+        device_id={"vocab": 1 - half}, device_id_type=MESH,
+    )
+    g_copy.start()
+
+    def head_of(ref, h):
+        return ref.at[:, pl.ds(pl.multiple_of(h * HEAD_DIM, HEAD_DIM), HEAD_DIM)]
+
+    def exchange(i, peer, source, target):
+        return pltpu.make_async_remote_copy(
+            src_ref=source, dst_ref=target.at[me],
+            send_sem=send_sem.at[i, peer], recv_sem=recv_sem.at[i, me],
+            device_id={"cp": peer}, device_id_type=MESH,
+        )
+
+    def input_copies(peer):
+        return (
+            exchange(0, peer, head_of(q_ref, peer), q_all),
+            exchange(1, peer, head_of(k_ref, peer // groups), k_all),
+            exchange(2, peer, head_of(v_ref, peer // groups), v_all),
+        )
+
+    def send_inputs(s, carry):
+        for copy in input_copies(lax.rem(me + s, n)):
+            copy.start()
+        return carry
+
+    lax.fori_loop(1, n, send_inputs, 0)
+    own_copies = (
+        pltpu.make_async_copy(head_of(q_ref, me), q_all.at[me], own_sem.at[0]),
+        pltpu.make_async_copy(head_of(k_ref, me // groups), k_all.at[me], own_sem.at[1]),
+        pltpu.make_async_copy(head_of(v_ref, me // groups), v_all.at[me], own_sem.at[2]),
+    )
+    for copy in own_copies:
+        copy.start()
+
+    own_g_copy.wait()
+
+    def first_half(s, carry):
+        t = lax.rem(s, pairs)
+        w_copy(t, True).wait()
+        partial[t] = dot(own_g[...], own_w[t], NT)
+        return carry
+
+    lax.fori_loop(1, pairs + 1, first_half, 0)
+    g_copy.wait()
+
+    def finish(t):
+        w_copy(t, False).wait()
+        u_buf[t] = (partial[t] + dot(other_g[...], other_w[t], NT)).astype(jnp.bfloat16)
+
+    def u_copy(t, peer, side):
+        return exchange(3, peer, head_of(u_buf.at[t], side), u_all)
+
+    def second_half(t, carry):
+        finish(t)
+        base = 2 * lax.rem(me // 2 + t, pairs)
+        u_copy(t, base, 0).start()
+        u_copy(t, base + 1, 1).start()
+        return carry
+
+    lax.fori_loop(1, pairs, second_half, 0)
+    finish(0)
+    side = lax.rem(me, 2)
+    buddy = me + 1 - 2 * side
+    u_copy(0, buddy, 1 - side).start()
+    own_u = pltpu.make_async_copy(head_of(u_buf.at[0], side), u_all.at[me], own_sem.at[3])
+    own_u.start()
+
+    def wait_all(s, carry):
+        sent = lax.rem(me + s, n)
+        source = lax.rem(me + n - s, n)
+        for i, target in enumerate((q_all, k_all, v_all, u_all)):
+            done = pltpu.make_async_remote_copy(
+                src_ref=target.at[source], dst_ref=target.at[source],
+                send_sem=send_sem.at[i, sent], recv_sem=recv_sem.at[i, source],
+                device_id={"cp": sent}, device_id_type=MESH,
+            )
+            done.wait_send()
+            done.wait_recv()
+        return carry
+
+    lax.fori_loop(1, n, wait_all, 0)
+    for copy in own_copies:
+        copy.wait()
+    own_u.wait()
+
+
+def attend_kernel(
+    order_ref, places_ref, q_ref, k_ref, v_ref, u_ref, dq_out, dkv_out,
+    qs, ks, vs, us, k_turned, s_buf, p_buf, dk_sum, dv_sum, dq_sum,
+):
+    seq = q_ref.shape[0]
+    spans = order_ref.shape[0]
+    rows = seq // spans
+    tiles = seq // TILE
+    factor = HEAD_DIM ** (-0.5)
+    scale = factor * 1.4426950408889634
+
+    for j in range(spans):
+        source = pl.ds(pl.multiple_of(places_ref[j] * rows, rows), rows)
+        for target, ref in ((qs, q_ref), (ks, k_ref), (vs, v_ref), (us, u_ref)):
+            target[pl.ds(j * rows, rows), :] = ref[source, :]
+    k_turned[...] = ks[...].T
+
+    def fold(x, op):
+        return op(x.reshape(TILE // 8, 8, TILE), axis=0)
+
+    key_at = lax.broadcasted_iota(jnp.int32, (TILE, TILE), 0)
+    query_at = lax.broadcasted_iota(jnp.int32, (TILE, TILE), 1)
+    for i in range(tiles):
+        own = pl.ds(i * TILE, TILE)
+        q_tile = qs[own, :]
+        u_tile = us[own, :]
+        peak = None
+        for j in range(i + 1):
+            keys = pl.ds(j * TILE, TILE)
+            s = dot(ks[keys, :], q_tile, NT)
+            if j == i:
+                s = jnp.where(key_at <= query_at, s, -1e30)
+            s_buf[keys, :] = s
+            top = fold(s, jnp.max)
+            peak = top if peak is None else jnp.maximum(peak, top)
+        peak = jnp.max(peak, axis=0, keepdims=True)
+        total = jnp.zeros((8, TILE), jnp.float32)
+        delta = jnp.zeros((8, TILE), jnp.float32)
+        for j in range(i + 1):
+            keys = pl.ds(j * TILE, TILE)
+            p = jnp.exp2((s_buf[keys, :] - peak) * scale)
+            dp = dot(vs[keys, :], u_tile, NT)
+            total = total + fold(p, jnp.sum)
+            delta = delta + fold(p * dp, jnp.sum)
+            s_buf[keys, :] = p
+            p_buf[keys, :] = dp
+        inverse = 1.0 / jnp.sum(total, axis=0, keepdims=True)
+        delta = jnp.sum(delta, axis=0, keepdims=True) * inverse
+        turned = None
+        for j in range(i + 1):
+            keys = pl.ds(j * TILE, TILE)
+            w = s_buf[keys, :] * inverse
+            g = (w * (p_buf[keys, :] - delta)).astype(jnp.bfloat16)
+            dk = dot(g, q_tile, NN)
+            dv = dot(w.astype(jnp.bfloat16), u_tile, NN)
+            if j == i:
+                dk_sum[keys, :] = dk
+                dv_sum[keys, :] = dv
+            else:
+                dk_sum[keys, :] += dk
+                dv_sum[keys, :] += dv
+            part = dot(k_turned[:, keys], g, NN)
+            turned = part if turned is None else turned + part
+        dq_sum[own, :] = turned.T
+
+    for r in range(spans):
+        source = pl.ds(pl.multiple_of(order_ref[r] * rows, rows), rows)
+        target = pl.ds(r * rows, rows)
+        dq_out[target, :] = (dq_sum[source, :] * factor).astype(jnp.bfloat16)
+        dkv_out[target, :HEAD_DIM] = (dk_sum[source, :] * factor).astype(jnp.bfloat16)
+        dkv_out[target, HEAD_DIM:] = dv_sum[source, :].astype(jnp.bfloat16)
+
+
+def return_kernel(n, dq_ref, dkv_ref, dq_all, dkv_all, send_sem, recv_sem, own_sem):
+    me = lax.axis_index("cp")
+    greet([{"cp": lax.rem(me + s, n)} for s in range(1, n)])
+    own_columns = pl.ds(pl.multiple_of(me * HEAD_DIM, HEAD_DIM), HEAD_DIM)
+
+    def copies(s):
+        peer = lax.rem(me + s, n)
+        return (
+            pltpu.make_async_remote_copy(
+                src_ref=dkv_ref.at[peer], dst_ref=dkv_all.at[me],
+                send_sem=send_sem.at[0, s], recv_sem=recv_sem.at[0, s],
+                device_id={"cp": peer}, device_id_type=MESH,
+            ),
+            pltpu.make_async_remote_copy(
+                src_ref=dq_ref.at[peer], dst_ref=dq_all.at[:, own_columns],
+                send_sem=send_sem.at[1, s], recv_sem=recv_sem.at[1, s],
+                device_id={"cp": peer}, device_id_type=MESH,
+            ),
+        )
+
+    def start(s, carry):
+        for copy in copies(s):
+            copy.start()
+        return carry
+
+    lax.fori_loop(1, n, start, 0)
+    own = (
+        pltpu.make_async_copy(dkv_ref.at[me], dkv_all.at[me], own_sem.at[0]),
+        pltpu.make_async_copy(dq_ref.at[me], dq_all.at[:, own_columns], own_sem.at[1]),
+    )
+    for copy in own:
+        copy.start()
+
+    def wait(s, carry):
+        for copy in copies(s):
+            copy.wait()
+        return carry
+
+    lax.fori_loop(1, n, wait, 0)
+    for copy in own:
+        copy.wait()
+
+
+def by_heads(n, queries, key_states, value_states, out_grad, o_weight, span_order):
+    own_rows, width = queries.shape
+    kv_heads = key_states.shape[1] // HEAD_DIM
+    groups = HEADS // KV_HEADS
+    seq = own_rows * n
+    pairs = n // 2
+    any_spec = pl.BlockSpec(memory_space=pl.ANY)
+    vmem_spec = pl.BlockSpec(memory_space=pltpu.VMEM)
+    smem_spec = pl.BlockSpec(memory_space=pltpu.SMEM)
+    dma = pltpu.SemaphoreType.DMA
+    low = jnp.bfloat16
+    block = jax.ShapeDtypeStruct((n, own_rows, HEAD_DIM), low)
+    gathered = pl.pallas_call(
+        functools.partial(send_kernel, n, groups),
+        out_shape=(block,) * 4,
+        in_specs=[any_spec] * 5,
+        out_specs=(vmem_spec,) * 4,
+        scratch_shapes=[
+            pltpu.VMEM((own_rows, width), low),
+            pltpu.VMEM((own_rows, width), low),
+            pltpu.VMEM((pairs, 2 * HEAD_DIM, width), low),
+            pltpu.VMEM((pairs, 2 * HEAD_DIM, width), low),
+            pltpu.VMEM((pairs, own_rows, 2 * HEAD_DIM), jnp.float32),
+            pltpu.VMEM((pairs, own_rows, 2 * HEAD_DIM), low),
+            dma((4, n)),
+            dma((4, n)),
+            dma((4,)),
+            dma((2, pairs)),
+            dma(()),
+            dma((2,)),
+        ],
+        compiler_params=pltpu.CompilerParams(
+            collective_id=0, has_side_effects=True, vmem_limit_bytes=40 << 20
+        ),
+        name="send_heads",
+    )(queries, key_states, value_states, out_grad, o_weight)
+    spans = span_order.shape[0]
+    ids = jnp.arange(spans, dtype=jnp.int32)
+    places = jnp.sum(
+        jnp.where(span_order[None, :] == ids[:, None], ids[None, :], 0), axis=1, dtype=jnp.int32
+    )
+    wide = pltpu.VMEM((seq, HEAD_DIM), jnp.float32)
+    dq, dkv = pl.pallas_call(
+        attend_kernel,
+        out_shape=(
+            jax.ShapeDtypeStruct((seq, HEAD_DIM), low),
+            jax.ShapeDtypeStruct((seq, 2 * HEAD_DIM), low),
+        ),
+        in_specs=[smem_spec] * 2 + [vmem_spec] * 4,
+        out_specs=(vmem_spec,) * 2,
+        scratch_shapes=[pltpu.VMEM((seq, HEAD_DIM), low)] * 4
+        + [pltpu.VMEM((HEAD_DIM, seq), low)]
+        + [pltpu.VMEM((seq, TILE), jnp.float32)] * 2
+        + [wide] * 3,
+        compiler_params=pltpu.CompilerParams(vmem_limit_bytes=40 << 20),
+        name="attend",
+    )(span_order, places, *(x.reshape(seq, HEAD_DIM) for x in gathered))
+    dq_all, dkv_all = pl.pallas_call(
+        functools.partial(return_kernel, n),
+        out_shape=(
+            jax.ShapeDtypeStruct((own_rows, width), low),
+            jax.ShapeDtypeStruct((n, own_rows, 2 * HEAD_DIM), low),
+        ),
+        in_specs=[any_spec] * 2,
+        out_specs=(vmem_spec,) * 2,
+        scratch_shapes=[dma((2, n)), dma((2, n)), dma((2,))],
+        compiler_params=pltpu.CompilerParams(
+            collective_id=1, has_side_effects=True, vmem_limit_bytes=16 << 20
+        ),
+        name="return_grads",
+    )(dq.reshape(n, own_rows, HEAD_DIM), dkv.reshape(n, own_rows, 2 * HEAD_DIM))
+    query_grad = dq_all.astype(jnp.float32)
+
+    def over_group(part):
+        heads = [
+            sum(part[g * groups + h].astype(jnp.float32) for h in range(groups))
+            for g in range(kv_heads)
+        ]
+        return jnp.concatenate(heads, axis=1)
+
+    return (
+        query_grad,
+        over_group(dkv_all[:, :, :HEAD_DIM]),
+        over_group(dkv_all[:, :, HEAD_DIM:]),
+    )
+
+
 def solution(mesh):
+    n = mesh.shape["cp"]
+    fits = mesh.shape["vocab"] == 2 and HEADS == 2 * n and n % 2 == 0
+    body = functools.partial(by_heads, n) if fits else local
     return jax.shard_map(
-        local,
+        body,
         mesh=mesh,
         in_specs=(
             P("cp", "vocab"),

time: 254 us -> 109 us (0.43); the launches traced: 250 us -> 108 us
  waiting for transfers between devices: 156 us -> 0 us
  Pallas kernels: 0 us -> 101 us
  matrix products: 40.6 us -> 0 us
  local copies, waits for them, and re-layouts: 31.1 us -> 3.89 us
  between operations: 13.9 us -> 0.7 us
  loops' own time: 3.08 us -> 0 us
  other arithmetic: 5.53 us -> 2.86 us
    pallas_call x0 -> x3, Pallas kernels: none -> 101 us  [the longest x1 51.6 us: by_heads(): pl.pallas_call(functools.partial(send_kernel, n, groups), out_shape=(bloc...]
    all_gather x3 -> x0, waiting for transfers between devices: 86.7 us -> none  [the longest x1 39.9 us: local(): lax.all_gather(value_states, 'cp', axis=0, tiled=True)]
    reduce_scatter x1 -> x0, waiting for transfers between devices: 68.6 us -> none  [local(): lax.psum_scatter(terms.astype(jnp.bfloat16), 'cp', scatter_dimension=0, t...]
    dot_general x15 -> x0, matrix products: 40.6 us -> none  [the longest x1 11.7 us: local(): lax.dot_general(lax.all_gather(out_grad, 'vocab', axis=1, tiled=True), o_...]
    unnamed x10, local copies, waits for them, and re-layouts: 14.9 us -> 3.89 us
    convert_element_type x1 -> x0, local copies, waits for them, and re-layouts: 6.24 us -> none  [local(): terms.astype(jnp.bfloat16)]
    while x30 -> x0, local copies, waits for them, and re-layouts: 3.94 us -> none
    another operation x2 -> x0, loops' own time: 3.08 us -> none  [the longest x1 1.59 us: local(): query_total, stacked = lax.scan(grad_step, query_zeros, block_ids)]
  transfers between devices with their start and end apart: 4 -> 0, of which waited for: 4 -> 0; matrix products, arithmetic and copies ran while one was open for 10% -> 0% of each run, Pallas kernels for 0% -> 0%
where the time goes in v1:
time: 109 us; the launch traced here: 108 us
  Pallas kernels  101 us (93%)
  local copies, waits for them, and re-layouts  3.89 us (4%)
  other arithmetic  2.86 us (3%)
    pallas_call x1, Pallas kernels, by_heads(): pl.pallas_call(functools.partial(send_kernel, n, groups), out_shape=(bloc...  51.6 us
    pallas_call x1, Pallas kernels, by_heads(): pl.pallas_call(functools.partial(return_kernel, n), out_shape=(jax.ShapeD...  38.9 us
    pallas_call x1, Pallas kernels, by_heads(): pl.pallas_call(attend_kernel, out_shape=(jax.ShapeDtypeStruct((seq, HEAD_...  10.3 us
    unnamed x10, local copies, waits for them, and re-layouts  3.89 us

profile of v1, /device:TPU:15, one launch (start us, length us, event | category | flops | bytes accessed | tf_op | source)
XLA Modules:
  0.0 108.2 jit_solution(11877799799690162082)
XLA Ops:
  0.6 0.0 copy-start.4
  0.6 0.8 select_reduce_fusion.places_ref
  1.5 0.0 copy-start
  1.5 1.0 copy-done
  2.5 0.0 copy-start.1
  2.5 1.0 copy-done.1
  3.6 0.0 copy-start.2
  3.6 0.9 copy-done.2
  4.5 0.0 copy-start.3
  4.5 0.9 copy-done.3
  5.4 51.6 %send_heads.1 = (bf16[16,128,128]{2,1,0:T(8,128)(2,1)S(1)}, bf16[16,128,128]{2,1,0:T(8,128)(2,1)S(1)}, bf16[16,128,128]{2,1,0:T(8,128)(2,1)S(1)}, bf16[16,128,128]{2,1,0:T(8,128)(2,1)S(1)}) custom-call(bf16[128,2048]{1,0:T(8,128)(2,1)S(1)} %copy-done, bf16[128,512]{1,0:T(8,128)(2,1)S(1)} %copy-done.2, bf16[128,512]{1,0:T(8,128)(2,1)S(1)} %copy-done.3, ...), custom_call_target="tpu_custom_call" | custom-call | tf_op jit(solution)/shard_map/send_heads/pallas_call | solution.py:405
  57.0 0.0 copy-done.4
  57.0 10.3 %attend.1 = (bf16[2048,128]{1,0:T(8,128)(2,1)S(1)}, bf16[2048,256]{1,0:T(8,128)(2,1)S(1)}) custom-call(s32[32]{0:T(128)S(1)} %copy-done.4, s32[32]{0:T(128)S(1)} %select_reduce_fusion.places_ref, bf16[2048,128]{1,0:T(8,128)(2,1)S(1)} %bitcast.24, bf16[2048,128]{1,0:T(8,128)(2,1)S(1)} %bitcast.25, bf16[2048,128]{1,0:T(8,128)(2,1)S(1)} %bitcast.26, ...), custom_call_target="tpu_custom_call" | custom-call | tf_op jit(solution)/shard_map/attend/pallas_call | solution.py:435
  67.3 38.9 %return_grads.1 = (bf16[128,2048]{1,0:T(8,128)(2,1)S(1)}, bf16[16,128,256]{2,1,0:T(8,128)(2,1)S(1)}) custom-call(bf16[16,128,128]{2,1,0:T(8,128)(2,1)S(1)} %bitcast.23, bf16[16,128,256]{2,1,0:T(8,128)(2,1)S(1)} %bitcast.22), custom_call_target="tpu_custom_call" | custom-call | tf_op jit(solution)/shard_map/return_grads/pallas_call | solution.py:450
  106.2 0.1 add_bitcast_fusion.2
  106.3 0.1 add_bitcast_fusion.3
  106.3 0.8 pad_maximum_fusion
  107.2 1.1 convert_element_type.131
Async XLA Ops:
  0.6 56.4 %copy-start.4 = (s32[32]{0:T(128)S(1)}, s32[32]{0:T(128)}, u32[]{:S(2)}) copy-start(s32[32]{0:T(128)} %order_ref.1) | copy-start | bytes 388
  1.5 1.0 copy-start
  2.5 1.0 copy-start.1
  3.6 0.9 copy-start.2
  4.5 0.9 copy-start.3

commit v2 on v0

--- a/solution.py
+++ b/solution.py
@@ -1,6 +1,10 @@
+import functools
+
 import jax
 import jax.numpy as jnp
 from jax import lax
+from jax.experimental import pallas as pl
+from jax.experimental.pallas import tpu as pltpu
 from jax.sharding import PartitionSpec as P
 
 HEADS = 32
@@ -131,9 +135,372 @@
     return (query_grad, key_grad, value_grad)
 
 
+MESH = pl.DeviceIdType.MESH
+NT = (((1,), (1,)), ((), ()))
+NN = (((1,), (0,)), ((), ()))
+TILE = 256
+
+
+def dot(a, b, dims):
+    return lax.dot_general(a, b, dims, preferred_element_type=jnp.float32)
+
+
+def greet(peers):
+    barrier = pltpu.get_barrier_semaphore()
+    for peer in peers:
+        pl.semaphore_signal(barrier, inc=1, device_id=peer, device_id_type=MESH)
+    pl.semaphore_wait(barrier, len(peers))
+
+
+def send_kernel(
+    n, kv_heads, q_ref, k_ref, v_ref, g_ref, w_ref, q_all, k_all, v_all, u_all,
+    own_g, other_g, own_w, other_w, partial, u_buf,
+    send_sem, recv_sem, q_sems, u_sems, own_sem, w_sem, g_sem, gx_sem,
+):
+    me = lax.axis_index("cp")
+    half = lax.axis_index("vocab")
+    mine = lax.rem(me, kv_heads)
+    plane = me - mine
+    width = g_ref.shape[1]
+    wide = width // kv_heads
+    cut = wide // 2
+    offsets = list(range(kv_heads // 2, kv_heads)) + list(range(kv_heads // 2 - 1, -1, -1))
+    steps = [(o, part) for o in offsets for part in range(2)]
+
+    def member(o):
+        return lax.rem(mine + o, kv_heads)
+
+    def w_copy(t, own):
+        o, part = steps[t]
+        side = half if own else 1 - half
+        return pltpu.make_async_copy(
+            w_ref.at[
+                pl.ds(pl.multiple_of(member(o) * wide + part * cut, cut), cut),
+                pl.ds(pl.multiple_of(side * width, width), width),
+            ],
+            (own_w if own else other_w).at[t],
+            w_sem.at[0 if own else 1, t],
+        )
+
+    own_g_copy = pltpu.make_async_copy(g_ref, own_g, g_sem)
+    own_g_copy.start()
+    for t in range(len(steps)):
+        w_copy(t, True).start()
+    for t in range(len(steps)):
+        w_copy(t, False).start()
+
+    greet([{"cp": lax.rem(me + s, n)} for s in range(1, n)] + [{"vocab": 1 - half}])
+
+    g_copy = pltpu.make_async_remote_copy(
+        src_ref=g_ref, dst_ref=other_g, send_sem=gx_sem.at[0], recv_sem=gx_sem.at[1],
+        device_id={"vocab": 1 - half}, device_id_type=MESH,
+    )
+    g_copy.start()
+
+    def columns(ref, at, size):
+        return ref.at[:, pl.ds(pl.multiple_of(at * size, size), size)]
+
+    def q_copy(o):
+        to = member(o)
+        return pltpu.make_async_remote_copy(
+            src_ref=columns(q_ref, to, wide), dst_ref=q_all.at[mine],
+            send_sem=q_sems.at[0, o], recv_sem=q_sems.at[1, o],
+            device_id={"cp": plane + to}, device_id_type=MESH,
+        )
+
+    def u_copy(t):
+        o, part = steps[t]
+        return pltpu.make_async_remote_copy(
+            src_ref=u_buf.at[t], dst_ref=u_all.at[mine, :, pl.ds(part * cut, cut)],
+            send_sem=u_sems.at[0, t], recv_sem=u_sems.at[1, t],
+            device_id={"cp": plane + member(o)}, device_id_type=MESH,
+        )
+
+    def kv_copies(s):
+        peer = lax.rem(me + s, n)
+        head = lax.rem(peer, kv_heads)
+        return [
+            pltpu.make_async_remote_copy(
+                src_ref=columns(source, head, HEAD_DIM), dst_ref=target.at[me],
+                send_sem=send_sem.at[i, s], recv_sem=recv_sem.at[i, s],
+                device_id={"cp": peer}, device_id_type=MESH,
+            )
+            for i, (source, target) in enumerate(((k_ref, k_all), (v_ref, v_all)))
+        ]
+
+    def start_kv(s, carry):
+        for copy in kv_copies(s):
+            copy.start()
+        return carry
+
+    for o in offsets[:-1]:
+        q_copy(o).start()
+    lax.fori_loop(1, n, start_kv, 0)
+    own_copies = [
+        pltpu.make_async_copy(columns(q_ref, mine, wide), q_all.at[mine], own_sem.at[0]),
+        pltpu.make_async_copy(columns(k_ref, mine, HEAD_DIM), k_all.at[me], own_sem.at[1]),
+        pltpu.make_async_copy(columns(v_ref, mine, HEAD_DIM), v_all.at[me], own_sem.at[2]),
+    ]
+    for copy in own_copies:
+        copy.start()
+
+    own_g_copy.wait()
+    for t in range(len(steps)):
+        w_copy(t, True).wait()
+        partial[t] = dot(own_g[...], own_w[t], NT)
+    g_copy.wait()
+    for t, (o, part) in enumerate(steps):
+        w_copy(t, False).wait()
+        block = (partial[t] + dot(other_g[...], other_w[t], NT)).astype(jnp.bfloat16)
+        if o == 0:
+            u_all[mine, :, pl.ds(part * cut, cut)] = block
+        else:
+            u_buf[t] = block
+            u_copy(t).start()
+
+    def wait_kv(s, carry):
+        for copy in kv_copies(s):
+            copy.wait()
+        return carry
+
+    lax.fori_loop(1, n, wait_kv, 0)
+    for o in offsets[:-1]:
+        q_copy(o).wait()
+    for t, (o, part) in enumerate(steps):
+        if o != 0:
+            u_copy(t).wait()
+    for copy in own_copies:
+        copy.wait()
+
+
+def attend_kernel(
+    order_ref, q_ref, k_ref, v_ref, u_ref, dq_out, dkv_out,
+    places, ks, vs, k_turned, s_buf, p_buf, dk_sum, dv_sum,
+):
+    plane = lax.axis_index("cp") // q_ref.shape[0]
+    own_rows = q_ref.shape[1]
+    groups = q_ref.shape[2] // HEAD_DIM
+    seq = k_ref.shape[0]
+    spans = order_ref.shape[0]
+    rows = seq // spans
+    tile = groups * rows
+    own_spans = q_ref.shape[0] * own_rows // rows
+    per_block = own_rows // rows
+    factor = HEAD_DIM ** (-0.5)
+    scale = factor * 1.4426950408889634
+
+    for r in range(spans):
+        places[order_ref[r]] = r
+    for j in range(spans):
+        source = pl.ds(pl.multiple_of(places[j] * rows, rows), rows)
+        for target, ref in ((ks, k_ref), (vs, v_ref)):
+            target[pl.ds(j * rows, rows), :] = ref[source, :]
+    k_turned[...] = ks[...].T
+    dk_sum[...] = jnp.zeros_like(dk_sum)
+    dv_sum[...] = jnp.zeros_like(dv_sum)
+
+    def fold(x, op):
+        return op(x.reshape(TILE // 8, 8, tile), axis=0)
+
+    key_at = lax.broadcasted_iota(jnp.int32, (TILE, tile), 0)
+    query_at = lax.rem(lax.broadcasted_iota(jnp.int32, (TILE, tile), 1), rows)
+
+    def one_span(t, carry):
+        block = t // per_block
+        own = pl.ds(pl.multiple_of(lax.rem(t, per_block) * rows, rows), rows)
+        start = order_ref[plane * own_spans + t] * rows
+
+        def stacked(ref):
+            return jnp.concatenate(
+                [ref[block, own, h * HEAD_DIM : (h + 1) * HEAD_DIM] for h in range(groups)], axis=0
+            )
+
+        def with_keys(last):
+            q_tile = stacked(q_ref)
+            u_tile = stacked(u_ref)
+            peak = None
+            for j in range(last + 1):
+                keys = pl.ds(j * TILE, TILE)
+                s = dot(ks[keys, :], q_tile, NT)
+                if j == last:
+                    s = jnp.where(key_at + (last * TILE - start) <= query_at, s, -1e30)
+                s_buf[keys, :] = s
+                top = fold(s, jnp.max)
+                peak = top if peak is None else jnp.maximum(peak, top)
+            peak = jnp.max(peak, axis=0, keepdims=True)
+            total = jnp.zeros((8, tile), jnp.float32)
+            delta = jnp.zeros((8, tile), jnp.float32)
+            for j in range(last + 1):
+                keys = pl.ds(j * TILE, TILE)
+                p = jnp.exp2((s_buf[keys, :] - peak) * scale)
+                dp = dot(vs[keys, :], u_tile, NT)
+                total = total + fold(p, jnp.sum)
+                delta = delta + fold(p * dp, jnp.sum)
+                s_buf[keys, :] = p
+                p_buf[keys, :] = dp
+            inverse = 1.0 / jnp.sum(total, axis=0, keepdims=True)
+            delta = jnp.sum(delta, axis=0, keepdims=True) * inverse
+            turned = None
+            for j in range(last + 1):
+                keys = pl.ds(j * TILE, TILE)
+                w = s_buf[keys, :] * inverse
+                g = (w * (p_buf[keys, :] - delta)).astype(jnp.bfloat16)
+                dk_sum[keys, :] += dot(g, q_tile, NN)
+                dv_sum[keys, :] += dot(w.astype(jnp.bfloat16), u_tile, NN)
+                part = dot(k_turned[:, keys], g, NN)
+                turned = part if turned is None else turned + part
+            dq = (turned.T * factor).astype(jnp.bfloat16)
+            for h in range(groups):
+                dq_out[block, own, h * HEAD_DIM : (h + 1) * HEAD_DIM] = dq[h * rows : (h + 1) * rows]
+
+        for last in range(seq // TILE):
+            pl.when(start // TILE == last)(functools.partial(with_keys, last))
+        return carry
+
+    lax.fori_loop(0, own_spans, one_span, 0)
+    for r in range(spans):
+        source = pl.ds(pl.multiple_of(order_ref[r] * rows, rows), rows)
+        target = pl.ds(r * rows, rows)
+        dkv_out[target, :HEAD_DIM] = (dk_sum[source, :] * factor).astype(jnp.bfloat16)
+        dkv_out[target, HEAD_DIM:] = dv_sum[source, :].astype(jnp.bfloat16)
+
+
+def return_kernel(n, kv_heads, dq_ref, dkv_ref, dq_all, dkv_all, send_sem, recv_sem, q_sems, own_sem):
+    me = lax.axis_index("cp")
+    mine = lax.rem(me, kv_heads)
+    plane = me - mine
+    wide = dq_ref.shape[2]
+    greet([{"cp": lax.rem(me + s, n)} for s in range(1, n)])
+    own_columns = pl.ds(pl.multiple_of(mine * wide, wide), wide)
+
+    def dkv_copy(s):
+        peer = lax.rem(me + s, n)
+        return pltpu.make_async_remote_copy(
+            src_ref=dkv_ref.at[peer], dst_ref=dkv_all.at[me],
+            send_sem=send_sem.at[s], recv_sem=recv_sem.at[s],
+            device_id={"cp": peer}, device_id_type=MESH,
+        )
+
+    def dq_copy(o):
+        to = lax.rem(mine + o, kv_heads)
+        return pltpu.make_async_remote_copy(
+            src_ref=dq_ref.at[to], dst_ref=dq_all.at[:, own_columns],
+            send_sem=q_sems.at[0, o], recv_sem=q_sems.at[1, o],
+            device_id={"cp": plane + to}, device_id_type=MESH,
+        )
+
+    def start(s, carry):
+        dkv_copy(s).start()
+        return carry
+
+    lax.fori_loop(1, n, start, 0)
+    for o in range(1, kv_heads):
+        dq_copy(o).start()
+    own = (
+        pltpu.make_async_copy(dkv_ref.at[me], dkv_all.at[me], own_sem.at[0]),
+        pltpu.make_async_copy(dq_ref.at[mine], dq_all.at[:, own_columns], own_sem.at[1]),
+    )
+    for copy in own:
+        copy.start()
+
+    def wait(s, carry):
+        dkv_copy(s).wait()
+        return carry
+
+    lax.fori_loop(1, n, wait, 0)
+    for o in range(1, kv_heads):
+        dq_copy(o).wait()
+    for copy in own:
+        copy.wait()
+
+
+def by_planes(n, queries, key_states, value_states, out_grad, o_weight, span_order):
+    own_rows, width = queries.shape
+    kv_heads = key_states.shape[1] // HEAD_DIM
+    wide = width // kv_heads
+    cut = wide // 2
+    seq = own_rows * n
+    tile = (HEADS // KV_HEADS) * (seq // span_order.shape[0])
+    hbm_spec = pl.BlockSpec(memory_space=pltpu.HBM)
+    vmem_spec = pl.BlockSpec(memory_space=pltpu.VMEM)
+    smem_spec = pl.BlockSpec(memory_space=pltpu.SMEM)
+    dma = pltpu.SemaphoreType.DMA
+    low = jnp.bfloat16
+    q_block = jax.ShapeDtypeStruct((kv_heads, own_rows, wide), low)
+    kv_block = jax.ShapeDtypeStruct((n, own_rows, HEAD_DIM), low)
+    q_all, k_all, v_all, u_all = pl.pallas_call(
+        functools.partial(send_kernel, n, kv_heads),
+        out_shape=(q_block, kv_block, kv_block, q_block),
+        in_specs=[hbm_spec] * 5,
+        out_specs=(vmem_spec,) * 4,
+        scratch_shapes=[
+            pltpu.VMEM((own_rows, width), low),
+            pltpu.VMEM((own_rows, width), low),
+            pltpu.VMEM((2 * kv_heads, cut, width), low),
+            pltpu.VMEM((2 * kv_heads, cut, width), low),
+            pltpu.VMEM((2 * kv_heads, own_rows, cut), jnp.float32),
+            pltpu.VMEM((2 * kv_heads, own_rows, cut), low),
+            dma((2, n)),
+            dma((2, n)),
+            dma((2, kv_heads)),
+            dma((2, 2 * kv_heads)),
+            dma((3,)),
+            dma((2, 2 * kv_heads)),
+            dma(()),
+            dma((2,)),
+        ],
+        compiler_params=pltpu.CompilerParams(
+            collective_id=0, has_side_effects=True, vmem_limit_bytes=40 << 20
+        ),
+        name="send_heads",
+    )(queries, key_states, value_states, out_grad, o_weight)
+    dq, dkv = pl.pallas_call(
+        attend_kernel,
+        out_shape=(q_block, jax.ShapeDtypeStruct((seq, 2 * HEAD_DIM), low)),
+        in_specs=[smem_spec] + [vmem_spec] * 4,
+        out_specs=(vmem_spec,) * 2,
+        scratch_shapes=[pltpu.SMEM(span_order.shape, jnp.int32)]
+        + [pltpu.VMEM((seq, HEAD_DIM), low)] * 2
+        + [pltpu.VMEM((HEAD_DIM, seq), low)]
+        + [pltpu.VMEM((seq, tile), jnp.float32)] * 2
+        + [pltpu.VMEM((seq, HEAD_DIM), jnp.float32)] * 2,
+        compiler_params=pltpu.CompilerParams(vmem_limit_bytes=40 << 20),
+        name="attend",
+    )(span_order, q_all, k_all.reshape(seq, HEAD_DIM), v_all.reshape(seq, HEAD_DIM), u_all)
+    dq_all, dkv_all = pl.pallas_call(
+        functools.partial(return_kernel, n, kv_heads),
+        out_shape=(
+            jax.ShapeDtypeStruct((own_rows, width), low),
+            jax.ShapeDtypeStruct((n, own_rows, 2 * HEAD_DIM), low),
+        ),
+        in_specs=[pl.BlockSpec(memory_space=pl.ANY)] * 2,
+        out_specs=(vmem_spec,) * 2,
+        scratch_shapes=[dma((n,)), dma((n,)), dma((2, kv_heads)), dma((2,))],
+        compiler_params=pltpu.CompilerParams(
+            collective_id=1, has_side_effects=True, vmem_limit_bytes=16 << 20
+        ),
+        name="return_grads",
+    )(dq, dkv.reshape(n, own_rows, 2 * HEAD_DIM))
+
+    def over_planes(part):
+        heads = [
+            sum(part[d].astype(jnp.float32) for d in range(g, n, kv_heads)) for g in range(kv_heads)
+        ]
+        return jnp.concatenate(heads, axis=1)
+
+    return (
+        dq_all.astype(jnp.float32),
+        over_planes(dkv_all[:, :, :HEAD_DIM]),
+        over_planes(dkv_all[:, :, HEAD_DIM:]),
+    )
+
+
 def solution(mesh):
+    n = mesh.shape["cp"]
+    planes = mesh.shape["vocab"] == 2 and n % (KV_HEADS // 2) == 0
+    body = functools.partial(by_planes, n) if planes else local
     return jax.shard_map(
-        local,
+        body,
         mesh=mesh,
         in_specs=(
             P("cp", "vocab"),

time: 254 us -> 76.2 us (0.30); the launches traced: 250 us -> 75.5 us
  waiting for transfers between devices: 156 us -> 0 us
  Pallas kernels: 0 us -> 68.9 us
  matrix products: 40.6 us -> 0 us
  local copies, waits for them, and re-layouts: 31.1 us -> 3.89 us
  between operations: 13.9 us -> 0.69 us
  other arithmetic: 5.53 us -> 2.03 us
  loops' own time: 3.08 us -> 0 us
    all_gather x3 -> x0, waiting for transfers between devices: 86.7 us -> none  [the longest x1 39.9 us: local(): lax.all_gather(value_states, 'cp', axis=0, tiled=True)]
    pallas_call x0 -> x3, Pallas kernels: none -> 68.9 us  [the longest x1 28.7 us: by_planes(): pl.pallas_call(functools.partial(send_kernel, n, kv_heads), out_shape=(q_...]
    reduce_scatter x1 -> x0, waiting for transfers between devices: 68.6 us -> none  [local(): lax.psum_scatter(terms.astype(jnp.bfloat16), 'cp', scatter_dimension=0, t...]
    dot_general x15 -> x0, matrix products: 40.6 us -> none  [the longest x1 11.7 us: local(): lax.dot_general(lax.all_gather(out_grad, 'vocab', axis=1, tiled=True), o_...]
    unnamed x10, local copies, waits for them, and re-layouts: 14.9 us -> 3.89 us
    convert_element_type x1 -> x0, local copies, waits for them, and re-layouts: 6.24 us -> none  [local(): terms.astype(jnp.bfloat16)]
    while x30 -> x0, local copies, waits for them, and re-layouts: 3.94 us -> none
    reduce_sum x2 -> x0, other arithmetic: 3.37 us -> none  [stats_step(): totals = totals * rescale + jnp.sum(raised, axis=3)]
  transfers between devices with their start and end apart: 4 -> 0, of which waited for: 4 -> 0; matrix products, arithmetic and copies ran while one was open for 10% -> 0% of each run, Pallas kernels for 0% -> 0%
where the time goes in v2:
time: 76.2 us; the launch traced here: 75.5 us
  Pallas kernels  68.9 us (90%)
  local copies, waits for them, and re-layouts  3.89 us (5%)
  other arithmetic  2.03 us (3%)
    pallas_call x1, Pallas kernels, by_planes(): pl.pallas_call(functools.partial(send_kernel, n, kv_heads), out_shape=(q_...  28.7 us
    pallas_call x1, Pallas kernels, by_planes(): pl.pallas_call(functools.partial(return_kernel, n, kv_heads), out_shape=(...  27.3 us
    pallas_call x1, Pallas kernels, by_planes(): pl.pallas_call(attend_kernel, out_shape=(q_block, jax.ShapeDtypeStruct((s...  12.9 us
    unnamed x10, local copies, waits for them, and re-layouts  3.89 us

profile of v2, /device:TPU:15, one launch (start us, length us, event | category | flops | bytes accessed | tf_op | source)
XLA Modules:
  0.0 75.5 jit_solution(4417446080423062039)
XLA Ops:
  0.6 0.0 copy-start
  0.6 1.0 %copy-done = bf16[128,2048]{1,0:T(8,128)(2,1)S(1)} copy-done((bf16[128,2048]{1,0:T(8,128)(2,1)S(1)}, bf16[128,2048]{1,0:T(8,128)(2,1)}, u32[]{:S(2)}) %copy-start) | copy-done | bytes 524312
  1.7 0.0 copy-start.1
  1.7 1.0 %copy-done.1 = bf16[128,2048]{1,0:T(8,128)(2,1)S(1)} copy-done((bf16[128,2048]{1,0:T(8,128)(2,1)S(1)}, bf16[128,2048]{1,0:T(8,128)(2,1)}, u32[]{:S(2)}) %copy-start.1) | copy-done | bytes 524312
  2.7 0.0 copy-start.2
  2.7 0.9 %copy-done.2 = bf16[128,512]{1,0:T(8,128)(2,1)S(1)} copy-done((bf16[128,512]{1,0:T(8,128)(2,1)S(1)}, bf16[128,512]{1,0:T(8,128)(2,1)}, u32[]{:S(2)}) %copy-start.2) | copy-done | bytes 131096
  3.6 0.0 copy-start.3
  3.6 0.9 %copy-done.3 = bf16[128,512]{1,0:T(8,128)(2,1)S(1)} copy-done((bf16[128,512]{1,0:T(8,128)(2,1)S(1)}, bf16[128,512]{1,0:T(8,128)(2,1)}, u32[]{:S(2)}) %copy-start.3) | copy-done | bytes 131096
  4.5 0.0 copy-start.4
  4.5 28.7 %send_heads.1 = (bf16[4,128,512]{2,1,0:T(8,128)(2,1)S(1)}, bf16[16,128,128]{2,1,0:T(8,128)(2,1)S(1)}, bf16[16,128,128]{2,1,0:T(8,128)(2,1)S(1)}, bf16[4,128,512]{2,1,0:T(8,128)(2,1)S(1)}) custom-call(bf16[128,2048]{1,0:T(8,128)(2,1)S(1)} %copy-done, bf16[128,512]{1,0:T(8,128)(2,1)S(1)} %copy-done.2, bf16[128,512]{1,0:T(8,128)(2,1)S(1)} %copy-done.3, ...), custom_call_target="tpu_custom_call" | custom-call | tf_op jit(solution)/shard_map/send_heads/pallas_call | solution.py:431
  33.3 0.0 copy-done.4
  33.3 12.9 %attend.1 = (bf16[4,128,512]{2,1,0:T(8,128)(2,1)S(1)}, bf16[2048,256]{1,0:T(8,128)(2,1)S(1)}) custom-call(s32[32]{0:T(128)S(1)} %copy-done.4, bf16[4,128,512]{2,1,0:T(8,128)(2,1)S(1)} %get-tuple-element.11.q_ref, bf16[2048,128]{1,0:T(8,128)(2,1)S(1)} %bitcast.20, bf16[2048,128]{1,0:T(8,128)(2,1)S(1)} %bitcast.21, ...), custom_call_target="tpu_custom_call" | custom-call | tf_op jit(solution)/shard_map/attend/pallas_call | solution.py:457
  46.2 27.3 %return_grads.1 = (bf16[128,2048]{1,0:T(8,128)(2,1)S(1)}, bf16[16,128,256]{2,1,0:T(8,128)(2,1)S(1)}) custom-call(bf16[4,128,512]{2,1,0:T(8,128)(2,1)S(1)} %get-tuple-element.15.dq_ref, bf16[16,128,256]{2,1,0:T(8,128)(2,1)S(1)} %bitcast.19), custom_call_target="tpu_custom_call" | custom-call | tf_op jit(solution)/shard_map/return_grads/pallas_call | solution.py:470
  73.5 0.1 add_bitcast_fusion.2
  73.5 0.1 add_bitcast_fusion.3
  73.6 0.8 %pad_maximum_fusion = (f32[128,512]{1,0:T(8,128)}, f32[128,512]{1,0:T(8,128)}) fusion(f32[128,128]{1,0:T(8,128)S(1)} %get-tuple-element.26, f32[128,128]{1,0:T(8,128)S(1)} %get-tuple-element.24, f32[128,128]{1,0:T(8,128)S(1)} %get-tuple-element.20, f32[128,128]{1,0:T(8,128)S(1)} %get-tuple-element.25, f32[128,128]{1,0:T(8,128)S(1)} %get-tuple-element.22, ...), kind=kLoop, calls=%fused_computation | loop fusion | flops 393216 | bytes 1048576 | tf_op jit(solution)/shard_map/concatenate | solution.py:489
  74.4 1.1 %convert_element_type.131 = f32[128,2048]{1,0:T(8,128)} convert(bf16[128,2048]{1,0:T(8,128)(2,1)S(1)} %get-tuple-element.17) | non-fusion elementwise | flops 262144 | bytes 1572864 | tf_op jit(solution)/shard_map/convert_element_type | solution.py:492
Async XLA Ops:
  0.6 1.0 %copy-start = (bf16[128,2048]{1,0:T(8,128)(2,1)S(1)}, bf16[128,2048]{1,0:T(8,128)(2,1)}, u32[]{:S(2)}) copy-start(bf16[128,2048]{1,0:T(8,128)(2,1)} %q_ref.1) | copy-start | bytes 1572868
  1.7 1.0 %copy-start.1 = (bf16[128,2048]{1,0:T(8,128)(2,1)S(1)}, bf16[128,2048]{1,0:T(8,128)(2,1)}, u32[]{:S(2)}) copy-start(bf16[128,2048]{1,0:T(8,128)(2,1)} %g_ref.1) | copy-start | bytes 1572868
  2.7 0.9 %copy-start.2 = (bf16[128,512]{1,0:T(8,128)(2,1)S(1)}, bf16[128,512]{1,0:T(8,128)(2,1)}, u32[]{:S(2)}) copy-start(bf16[128,512]{1,0:T(8,128)(2,1)} %k_ref.1) | copy-start | bytes 393220
  3.6 0.9 %copy-start.3 = (bf16[128,512]{1,0:T(8,128)(2,1)S(1)}, bf16[128,512]{1,0:T(8,128)(2,1)}, u32[]{:S(2)}) copy-start(bf16[128,512]{1,0:T(8,128)(2,1)} %v_ref.1) | copy-start | bytes 393220
  4.5 28.7 %copy-start.4 = (s32[32]{0:T(128)S(1)}, s32[32]{0:T(128)}, u32[]{:S(2)}) copy-start(s32[32]{0:T(128)} %order_ref.1) | copy-start | bytes 388

commit v3 on v2

--- a/solution.py
+++ b/solution.py
@@ -365,53 +365,82 @@
         dkv_out[target, HEAD_DIM:] = dv_sum[source, :].astype(jnp.bfloat16)
 
 
-def return_kernel(n, kv_heads, dq_ref, dkv_ref, dq_all, dkv_all, send_sem, recv_sem, q_sems, own_sem):
+def return_kernel(
+    kv_heads, dq_ref, dkv_ref, dq_all, dkv_all,
+    relay, summed, send_sem, recv_sem, relay_sems, q_sems, own_sem,
+):
     me = lax.axis_index("cp")
     mine = lax.rem(me, kv_heads)
-    plane = me - mine
+    plane = me // kv_heads
+    pair = plane + 1 - 2 * lax.rem(plane, 2)
+    across = lax.rem(plane + 2, 4)
+    pair_across = lax.rem(pair + 2, 4)
     wide = dq_ref.shape[2]
+    n = 4 * kv_heads
     greet([{"cp": lax.rem(me + s, n)} for s in range(1, n)])
     own_columns = pl.ds(pl.multiple_of(mine * wide, wide), wide)
 
-    def dkv_copy(s):
-        peer = lax.rem(me + s, n)
+    def relay_copy(m):
         return pltpu.make_async_remote_copy(
-            src_ref=dkv_ref.at[peer], dst_ref=dkv_all.at[me],
-            send_sem=send_sem.at[s], recv_sem=recv_sem.at[s],
-            device_id={"cp": peer}, device_id_type=MESH,
-        )
+            src_ref=dkv_ref.at[pair_across * kv_heads + m], dst_ref=relay.at[m],
+            send_sem=relay_sems.at[0, m], recv_sem=relay_sems.at[1, m],
+            device_id={"cp": pair * kv_heads + mine}, device_id_type=MESH,
+        )
+
+    def dkv_copy(kind, m, source):
+        to = (plane, pair, across)[kind] * kv_heads + m
+        return pltpu.make_async_remote_copy(
+            src_ref=dkv_ref.at[to] if source is None else source,
+            dst_ref=dkv_all.at[kind * kv_heads + mine],
+            send_sem=send_sem.at[kind, m], recv_sem=recv_sem.at[kind, mine],
+            device_id={"cp": to}, device_id_type=MESH,
+        )
+
+    def arrived(kind, g):
+        slot = dkv_all.at[kind * kv_heads + g]
+        pltpu.make_async_remote_copy(
+            src_ref=slot, dst_ref=slot,
+            send_sem=send_sem.at[kind, g], recv_sem=recv_sem.at[kind, g],
+            device_id={"cp": pair * kv_heads + mine}, device_id_type=MESH,
+        ).wait_recv()
 
     def dq_copy(o):
         to = lax.rem(mine + o, kv_heads)
         return pltpu.make_async_remote_copy(
             src_ref=dq_ref.at[to], dst_ref=dq_all.at[:, own_columns],
             send_sem=q_sems.at[0, o], recv_sem=q_sems.at[1, o],
-            device_id={"cp": plane + to}, device_id_type=MESH,
-        )
-
-    def start(s, carry):
-        dkv_copy(s).start()
-        return carry
-
-    lax.fori_loop(1, n, start, 0)
+            device_id={"cp": plane * kv_heads + to}, device_id_type=MESH,
+        )
+
+    others = [lax.rem(mine + o, kv_heads) for o in range(1, kv_heads)]
+    for m in range(kv_heads):
+        relay_copy(m).start()
     for o in range(1, kv_heads):
         dq_copy(o).start()
-    own = (
-        pltpu.make_async_copy(dkv_ref.at[me], dkv_all.at[me], own_sem.at[0]),
-        pltpu.make_async_copy(dq_ref.at[mine], dq_all.at[:, own_columns], own_sem.at[1]),
-    )
-    for copy in own:
-        copy.start()
-
-    def wait(s, carry):
-        dkv_copy(s).wait()
-        return carry
-
-    lax.fori_loop(1, n, wait, 0)
+    own = pltpu.make_async_copy(dq_ref.at[mine], dq_all.at[:, own_columns], own_sem)
+    own.start()
+    for m in range(kv_heads):
+        relay_copy(m).wait_recv()
+        total = dkv_ref[across * kv_heads + m].astype(jnp.float32) + relay[m].astype(jnp.float32)
+        summed[m] = total.astype(jnp.bfloat16)
+        dkv_copy(2, m, summed.at[m]).start()
+        dkv_copy(1, m, None).start()
+    for m in others:
+        dkv_copy(0, m, None).start()
+    dkv_all[mine] = dkv_ref[me]
+
+    for m in range(kv_heads):
+        relay_copy(m).wait_send()
+        dkv_copy(2, m, summed.at[m]).wait_send()
+        dkv_copy(1, m, None).wait_send()
+        arrived(1, m)
+        arrived(2, m)
+    for m in others:
+        dkv_copy(0, m, None).wait_send()
+        arrived(0, m)
     for o in range(1, kv_heads):
         dq_copy(o).wait()
-    for copy in own:
-        copy.wait()
+    own.wait()
 
 
 def by_planes(n, queries, key_states, value_states, out_grad, o_weight, span_order):
@@ -467,24 +496,32 @@
         compiler_params=pltpu.CompilerParams(vmem_limit_bytes=40 << 20),
         name="attend",
     )(span_order, q_all, k_all.reshape(seq, HEAD_DIM), v_all.reshape(seq, HEAD_DIM), u_all)
+    term = (own_rows, 2 * HEAD_DIM)
     dq_all, dkv_all = pl.pallas_call(
-        functools.partial(return_kernel, n, kv_heads),
+        functools.partial(return_kernel, kv_heads),
         out_shape=(
             jax.ShapeDtypeStruct((own_rows, width), low),
-            jax.ShapeDtypeStruct((n, own_rows, 2 * HEAD_DIM), low),
+            jax.ShapeDtypeStruct((3 * kv_heads,) + term, low),
         ),
-        in_specs=[pl.BlockSpec(memory_space=pl.ANY)] * 2,
+        in_specs=[pl.BlockSpec(memory_space=pl.ANY), vmem_spec],
         out_specs=(vmem_spec,) * 2,
-        scratch_shapes=[dma((n,)), dma((n,)), dma((2, kv_heads)), dma((2,))],
+        scratch_shapes=[pltpu.VMEM((kv_heads,) + term, low)] * 2
+        + [
+            dma((3, kv_heads)),
+            dma((3, kv_heads)),
+            dma((2, kv_heads)),
+            dma((2, kv_heads)),
+            dma(()),
+        ],
         compiler_params=pltpu.CompilerParams(
             collective_id=1, has_side_effects=True, vmem_limit_bytes=16 << 20
         ),
         name="return_grads",
-    )(dq, dkv.reshape(n, own_rows, 2 * HEAD_DIM))
+    )(dq, dkv.reshape((n,) + term))
 
     def over_planes(part):
         heads = [
-            sum(part[d].astype(jnp.float32) for d in range(g, n, kv_heads)) for g in range(kv_heads)
+            sum(part[d].astype(jnp.float32) for d in range(g, 3 * kv_heads, kv_heads)) for g in range(kv_heads)
         ]
         return jnp.concatenate(heads, axis=1)
 
@@ -497,7 +534,7 @@
 
 def solution(mesh):
     n = mesh.shape["cp"]
-    planes = mesh.shape["vocab"] == 2 and n % (KV_HEADS // 2) == 0
+    planes = mesh.shape["vocab"] == 2 and n == 4 * (KV_HEADS // 2)
     body = functools.partial(by_planes, n) if planes else local
     return jax.shard_map(
         body,

time: 76.2 us -> 71.8 us (0.942)
  Pallas kernels: 68.9 us -> 63.9 us
    pallas_call x1, Pallas kernels: 27.3 us -> 23.8 us  [by_planes(): pl.pallas_call(functools.partial(return_kernel, kv_heads), out_shape=(jax...]
    pallas_call x1, Pallas kernels: 12.9 us -> 11.4 us  [by_planes(): pl.pallas_call(attend_kernel, out_shape=(q_block, jax.ShapeDtypeStruct((s...]
where the time goes in v3:
time: 71.8 us; the launch traced here: 70.5 us
  Pallas kernels  63.9 us (89%)
  local copies, waits for them, and re-layouts  3.89 us (5%)
  other arithmetic  2 us (3%)
    pallas_call x1, Pallas kernels, by_planes(): pl.pallas_call(functools.partial(send_kernel, n, kv_heads), out_shape=(q_...  28.7 us
    pallas_call x1, Pallas kernels, by_planes(): pl.pallas_call(functools.partial(return_kernel, kv_heads), out_shape=(jax...  23.8 us
    pallas_call x1, Pallas kernels, by_planes(): pl.pallas_call(attend_kernel, out_shape=(q_block, jax.ShapeDtypeStruct((s...  11.4 us
    unnamed x10, local copies, waits for them, and re-layouts  3.89 us

profile of v3, /device:TPU:15, one launch (start us, length us, event | category | flops | bytes accessed | tf_op | source)
XLA Modules:
  0.0 70.5 jit_solution(15639688251941472884)
XLA Ops:
  0.6 0.0 copy-start
  0.6 1.0 %copy-done = bf16[128,2048]{1,0:T(8,128)(2,1)S(1)} copy-done((bf16[128,2048]{1,0:T(8,128)(2,1)S(1)}, bf16[128,2048]{1,0:T(8,128)(2,1)}, u32[]{:S(2)}) %copy-start) | copy-done | bytes 524312
  1.7 0.0 copy-start.1
  1.7 1.0 %copy-done.1 = bf16[128,2048]{1,0:T(8,128)(2,1)S(1)} copy-done((bf16[128,2048]{1,0:T(8,128)(2,1)S(1)}, bf16[128,2048]{1,0:T(8,128)(2,1)}, u32[]{:S(2)}) %copy-start.1) | copy-done | bytes 524312
  2.7 0.0 copy-start.2
  2.7 0.9 %copy-done.2 = bf16[128,512]{1,0:T(8,128)(2,1)S(1)} copy-done((bf16[128,512]{1,0:T(8,128)(2,1)S(1)}, bf16[128,512]{1,0:T(8,128)(2,1)}, u32[]{:S(2)}) %copy-start.2) | copy-done | bytes 131096
  3.6 0.0 copy-start.3
  3.6 0.9 %copy-done.3 = bf16[128,512]{1,0:T(8,128)(2,1)S(1)} copy-done((bf16[128,512]{1,0:T(8,128)(2,1)S(1)}, bf16[128,512]{1,0:T(8,128)(2,1)}, u32[]{:S(2)}) %copy-start.3) | copy-done | bytes 131096
  4.5 0.0 copy-start.4
  4.5 28.7 %send_heads.1 = (bf16[4,128,512]{2,1,0:T(8,128)(2,1)S(1)}, bf16[16,128,128]{2,1,0:T(8,128)(2,1)S(1)}, bf16[16,128,128]{2,1,0:T(8,128)(2,1)S(1)}, bf16[4,128,512]{2,1,0:T(8,128)(2,1)S(1)}) custom-call(bf16[128,2048]{1,0:T(8,128)(2,1)S(1)} %copy-done, bf16[128,512]{1,0:T(8,128)(2,1)S(1)} %copy-done.2, bf16[128,512]{1,0:T(8,128)(2,1)S(1)} %copy-done.3, ...), custom_call_target="tpu_custom_call" | custom-call | tf_op jit(solution)/shard_map/send_heads/pallas_call | solution.py:460
  33.3 0.0 copy-done.4
  33.3 11.4 %attend.1 = (bf16[4,128,512]{2,1,0:T(8,128)(2,1)S(1)}, bf16[2048,256]{1,0:T(8,128)(2,1)S(1)}) custom-call(s32[32]{0:T(128)S(1)} %copy-done.4, bf16[4,128,512]{2,1,0:T(8,128)(2,1)S(1)} %get-tuple-element.11.q_ref, bf16[2048,128]{1,0:T(8,128)(2,1)S(1)} %bitcast.20, bf16[2048,128]{1,0:T(8,128)(2,1)S(1)} %bitcast.21, ...), custom_call_target="tpu_custom_call" | custom-call | tf_op jit(solution)/shard_map/attend/pallas_call | solution.py:486
  44.7 23.8 %return_grads.1 = (bf16[128,2048]{1,0:T(8,128)(2,1)S(1)}, bf16[12,128,256]{2,1,0:T(8,128)(2,1)S(1)}) custom-call(bf16[4,128,512]{2,1,0:T(8,128)(2,1)S(1)} %get-tuple-element.15.dq_ref, bf16[16,128,256]{2,1,0:T(8,128)(2,1)S(1)} %bitcast.19), custom_call_target="tpu_custom_call" | custom-call | tf_op jit(solution)/shard_map/return_grads/pallas_call | solution.py:500
  68.5 0.1 add_bitcast_fusion.3
  68.6 0.8 %pad_maximum_fusion = (f32[128,512]{1,0:T(8,128)}, f32[128,512]{1,0:T(8,128)}) fusion(f32[128,128]{1,0:T(8,128)S(1)} %get-tuple-element.23, f32[128,128]{1,0:T(8,128)S(1)} %get-tuple-element.26, f32[128,128]{1,0:T(8,128)S(1)} %get-tuple-element.22, f32[128,128]{1,0:T(8,128)S(1)} %get-tuple-element.25, f32[128,128]{1,0:T(8,128)S(1)} %get-tuple-element.21, ...), kind=kLoop, calls=%fused_computation | loop fusion | flops 393216 | bytes 1048576 | tf_op jit(solution)/shard_map/concatenate | solution.py:526
  69.4 1.1 %convert_element_type.99 = f32[128,2048]{1,0:T(8,128)} convert(bf16[128,2048]{1,0:T(8,128)(2,1)S(1)} %get-tuple-element.17) | non-fusion elementwise | flops 262144 | bytes 1572864 | tf_op jit(solution)/shard_map/convert_element_type | solution.py:529
  (1 shorter events, 0.0 us)
Async XLA Ops:
  0.6 1.0 %copy-start = (bf16[128,2048]{1,0:T(8,128)(2,1)S(1)}, bf16[128,2048]{1,0:T(8,128)(2,1)}, u32[]{:S(2)}) copy-start(bf16[128,2048]{1,0:T(8,128)(2,1)} %q_ref.1) | copy-start | bytes 1572868
  1.7 1.0 %copy-start.1 = (bf16[128,2048]{1,0:T(8,128)(2,1)S(1)}, bf16[128,2048]{1,0:T(8,128)(2,1)}, u32[]{:S(2)}) copy-start(bf16[128,2048]{1,0:T(8,128)(2,1)} %g_ref.1) | copy-start | bytes 1572868
  2.7 0.9 %copy-start.2 = (bf16[128,512]{1,0:T(8,128)(2,1)S(1)}, bf16[128,512]{1,0:T(8,128)(2,1)}, u32[]{:S(2)}) copy-start(bf16[128,512]{1,0:T(8,128)(2,1)} %k_ref.1) | copy-start | bytes 393220
  3.6 0.9 %copy-start.3 = (bf16[128,512]{1,0:T(8,128)(2,1)S(1)}, bf16[128,512]{1,0:T(8,128)(2,1)}, u32[]{:S(2)}) copy-start(bf16[128,512]{1,0:T(8,128)(2,1)} %v_ref.1) | copy-start | bytes 393220
  4.5 28.7 %copy-start.4 = (s32[32]{0:T(128)S(1)}, s32[32]{0:T(128)}, u32[]{:S(2)}) copy-start(s32[32]{0:T(128)} %order_ref.1) | copy-start | bytes 388
